TPU v7x, 128 devices: a whole 4x4x4 slice. The times are simulated.
128 devices in a mesh: freq: 8 (over x, z_hi), panel: 16 (over z_lo, y, core).
Axes of the slice: x: 4, y: 4, z: 4 (z_hi: 2, z_lo: 2; z = z_hi * 2 + z_lo), core: 2. Of those that a mesh axis runs over, the one named last changes fastest.
Arguments:
- traces: bfloat16 [640, 640, 1024], P('panel', 'freq'), may hold values from -6 to 6
- filters: float32 [16, 7, 64], replicated, may hold values from -0.25 to 0.25
Outputs:
- primaries: bfloat16 [640, 640, 1024], P('panel', 'freq')
All inputs are finite; a program needn't handle non-finite values.
Results may differ from a plain program's by a relative error of at most 0.0095.
Values may be sent and summed in bfloat16 or wider, within the bound.
No kernel may reach another device: no remote copies, remote signals or barrier semaphores. Data moves between devices by JAX's collectives and lax.ppermute only.
A program may use at most 128 MiB of HBM per device.

v0:
```python
import math
import jax
import jax.numpy as jnp
from jax import lax
from jax.sharding import PartitionSpec as P

NS = 640
NT = 1024
NF = 96
FLO = 8
TAPS = 64
SPAN = 7
RWIN = 40


def wave_table(freq_bins, sample_index):
    phases = freq_bins[:, None] * sample_index[None, :] % NT
    angles = phases.astype(jnp.float32) * jnp.float32(2.0 * math.pi / NT)
    return (jnp.cos(angles), jnp.sin(angles))


def complex_product(left_side, right_side):

    def factor_product(leading_factor, trailing_factor):
        return jnp.einsum(
            "gjo,god->gjd", leading_factor, trailing_factor, preferred_element_type=jnp.float32
        )

    part_real = factor_product(left_side[0], right_side[0]) - factor_product(
        left_side[1], right_side[1]
    )
    part_imag = factor_product(left_side[0], right_side[1]) + factor_product(
        left_side[1], right_side[0]
    )
    return jnp.stack([part_real, part_imag])


def response(filters, freq_bins):
    tap_index = jnp.arange(TAPS, dtype=jnp.int32)
    cosine_wave, sine_wave = wave_table(freq_bins, tap_index)
    filter_real = jnp.einsum("fk,wjk->fjw", cosine_wave, filters)
    filter_imag = -jnp.einsum("fk,wjk->fjw", sine_wave, filters)
    return (jnp.repeat(filter_real, RWIN, axis=2), jnp.repeat(filter_imag, RWIN, axis=2))


def apply_filter(extended, filter_real, filter_imag, source_count):
    sum_real = jnp.zeros(extended.shape[1:2] + (source_count,) + extended.shape[3:], jnp.float32)
    sum_imag = jnp.zeros_like(sum_real)
    for shifted in range(SPAN):
        part_real = extended[0, :, shifted : shifted + source_count, :]
        part_imag = extended[1, :, shifted : shifted + source_count, :]
        weight_real = filter_real[:, shifted][:, None, :]
        weight_imaginary = filter_imag[:, shifted][:, None, :]
        sum_real = sum_real + weight_real * part_real - weight_imaginary * part_imag
        sum_imag = sum_imag + weight_real * part_imag + weight_imaginary * part_real
    return jnp.stack([sum_real, sum_imag])


def per_device(traces, filters):
    shot_rows, receiver_cols, time_sample_count = traces.shape
    rim_width = SPAN // 2
    scale_sources = jnp.float32(math.sqrt(NS))
    freq_bins = FLO + jnp.arange(NF, dtype=jnp.int32)
    cosine_wave, sine_wave = wave_table(freq_bins, jnp.arange(NT, dtype=jnp.int32))
    forward = (jnp.concatenate([cosine_wave, -sine_wave], 0) / jnp.float32(math.sqrt(NT))).astype(
        jnp.bfloat16
    )
    reciprocal_value = jnp.concatenate([cosine_wave, -sine_wave], 0).astype(jnp.bfloat16)
    spectra = jnp.einsum("srt,ct->csr", traces, forward, preferred_element_type=jnp.float32)
    spectra = spectra.astype(jnp.bfloat16).reshape(2, NF, shot_rows, receiver_cols)
    columns = lax.all_to_all(spectra, "panel", split_axis=1, concat_axis=2, tiled=True)
    slice_count = columns.shape[1]
    first_slice = lax.axis_index("panel") * slice_count
    complete = lax.all_gather(columns, "freq", axis=3, tiled=True)
    order_one = (complex_product(complete, columns) / scale_sources).astype(jnp.bfloat16)
    order_two = complex_product(complete, order_one) / scale_sources
    prediction = (order_one.astype(jnp.float32) - order_two).astype(jnp.bfloat16)
    extended = jnp.pad(
        prediction.astype(jnp.float32), ((0, 0), (0, 0), (rim_width, rim_width), (0, 0))
    )
    own_bins = FLO + first_slice + jnp.arange(slice_count, dtype=jnp.int32)
    filter_real, filter_imag = response(filters, own_bins)
    receiver_start = lax.axis_index("freq") * receiver_cols
    filter_real = lax.dynamic_slice_in_dim(filter_real, receiver_start, receiver_cols, 2)
    filter_imag = lax.dynamic_slice_in_dim(filter_imag, receiver_start, receiver_cols, 2)
    matched = apply_filter(extended, filter_real, filter_imag, NS)
    returned = lax.all_to_all(
        matched.astype(jnp.bfloat16), "panel", split_axis=2, concat_axis=1, tiled=True
    )
    matched_rows = returned.reshape(2 * NF, shot_rows, receiver_cols)
    multiples = jnp.einsum(
        "csr,ct->srt", matched_rows, reciprocal_value, preferred_element_type=jnp.float32
    )
    multiples = multiples / jnp.float32(math.sqrt(NF))
    return (traces.astype(jnp.float32) - multiples).astype(jnp.bfloat16)


def solution(mesh):
    placed = (P("panel", "freq", None), P())
    return jax.shard_map(
        per_device, mesh=mesh, in_specs=placed, out_specs=P("panel", "freq", None), check_vma=False
    )
```

profile of v0, /device:TPU:1, one launch (start us, length us, event | category | flops | bytes accessed | tf_op | source)
XLA Modules:
  0.0 312.2 jit_solution(14349941599640643925)
XLA Ops:
  6.5 1.6 fusion.58
  8.2 0.8 copy-done.4
  9.1 4.8 %convolution_convert_fusion = bf16[192,40,80]{0,2,1:T(8,128)(2,1)S(1)} fusion(bf16[40,80,1024]{2,1,0:T(8,128)(2,1)} %param.2, f32[96,1024]{1,0:T(8,128)S(1)} %get-tuple-element.24, f32[96,1024]{1,0:T(8,128)S(1)} %get-tuple-element.23), kind=kOutput, calls=%fused_computation.35 | convolution fusion | flops 1259495424 | bytes 8568832 | tf_op jit(solution)/shard_map/srt,ct->csr/dot_general | solution.py:69
  13.9 0.9 reshape.26
  14.7 3.3 %copy.54 = bf16[2,96,40,80]{3,2,0,1:T(8,128)(2,1)} copy(bf16[2,96,40,80]{1,0,3,2:T(2,128)(2,1)S(1)} %reshape.26) | data formatting | bytes 2457600 | tf_op jit(solution)/shard_map/reshape | solution.py:70
  18.1 32.3 %all_to_all.33 = bf16[2,96,40,80]{3,2,0,1:T(8,128)(2,1)S(1)} all-to-all(bf16[2,96,40,80]{3,2,0,1:T(8,128)(2,1)} %copy.54), channel_id=1, replica_groups=mesh['freq'=8,'panel'=16] {'panel'}, dimensions={1} | all-to-all | bytes 2457600 | tf_op jit(solution)/shard_map/all_to_all | solution.py:71
  50.4 1.7 copy.56
  52.2 4.5 %copy.57 = bf16[2,6,640,80]{2,0,1,3:T(2,128)(2,1)} copy(bf16[2,6,640,80]{3,2,1,0:T(8,128)(2,1)} %bitcast.140) | data formatting | bytes 2457600 | tf_op jit(solution)/shard_map/all_to_all | solution.py:71
  58.4 0.3 copy.55
  58.7 0.3 fusion.81
  59.3 118.6 %all-gather.2.cloned.1.call-done = bf16[2,6,640,640]{2,0,1,3:T(2,128)(2,1)} async-done(((bf16[2,6,640,80]{2,0,1,3:T(2,128)(2,1)}), bf16[2,6,640,640]{2,0,1,3:T(2,128)(2,1)}) %all-gather.2.cloned.1.call-update) | async-done | bytes 9830416 | tf_op jit(solution)/shard_map/all_gather | solution.py:74
  177.9 20.6 %fusion.80 = (bf16[1,6,640,640]{2,0,1,3:T(2,128)(2,1)}, bf16[1,6,640,640]{2,0,1,3:T(2,128)(2,1)}) fusion(bf16[2,6,640,640]{2,0,1,3:T(2,128)(2,1)} %all-gather.2.cloned.1.call-done), kind=kLoop, calls=%fused_computation.122 | loop fusion | bytes 19660800 | tf_op jit(solution)/shard_map/slice | solution.py:29
  198.5 19.7 %copy.91 = bf16[1,6,640,640]{3,2,1,0:T(8,128)(2,1)} copy(bf16[1,6,640,640]{2,0,1,3:T(2,128)(2,1)} %get-tuple-element.6) | data formatting | bytes 9830400
  218.3 19.8 %copy.90 = bf16[1,6,640,640]{3,2,1,0:T(8,128)(2,1)} copy(bf16[1,6,640,640]{2,0,1,3:T(2,128)(2,1)} %get-tuple-element.5) | data formatting | bytes 9830400
  238.0 4.2 %fusion.6 = f32[6,640,80]{1,2,0:T(8,128)S(1)} fusion(bf16[6,640,80]{2,1,0:T(8,128)(2,1)S(1)} %bitcast.133, bf16[1,6,640,640]{3,2,1,0:T(8,128)(2,1)} %copy.91), kind=kOutput, calls=%fused_computation.7 | convolution fusion | flops 393216000 | bytes 6758400 | tf_op jit(solution)/shard_map/gjo,god->gjd/dot_general | solution.py:25
  242.2 1.7 fusion.4
  243.9 0.7 copy-done.3
  244.6 1.7 fusion.23
  246.3 1.7 fusion.29
  248.2 1.7 fusion.2
  249.8 1.7 fusion
  251.5 1.7 fusion.35
  253.2 1.7 fusion.41
  254.8 0.4 fusion.44
  255.2 5.4 %subtract_convert_fusion.1 = bf16[1,6,640,80]{2,3,1,0:T(8,128)(2,1)S(1)} fusion(f32[2,6,640,80]{2,3,1,0:T(8,128)S(1)} %fusion.44, f32[6,80]{1,0:T(8,128)S(1)} %bitcast.143, f32[6,80]{1,0:T(8,128)S(1)} %bitcast.145, f32[6,80]{1,0:T(8,128)S(1)} %bitcast.147, f32[6,80]{1,0:T(8,128)S(1)} %bitcast.149, f32[6,80]{1,0:T(8,128)S(1)} %bitcast.151, ...), kind=kLoop, calls=%fused_computation.47 | loop fusion | flops 8601600 | bytes 5586944 | tf_op jit(solution)/shard_map/convert
  260.6 5.3 %add_convert_fusion = bf16[1,6,640,80]{2,3,1,0:T(8,128)(2,1)S(1)} fusion(f32[2,6,640,80]{2,3,1,0:T(8,128)S(1)} %fusion.44, f32[6,80]{1,0:T(8,128)S(1)} %bitcast.144, f32[6,80]{1,0:T(8,128)S(1)} %bitcast.146, f32[6,80]{1,0:T(8,128)S(1)} %bitcast.148, f32[6,80]{1,0:T(8,128)S(1)} %bitcast.150, f32[6,80]{1,0:T(8,128)S(1)} %bitcast.152, ...), kind=kLoop, calls=%fused_computation.46 | loop fusion | flops 8601600 | bytes 5586944 | tf_op jit(solution)/shard_map/convert.1
  266.1 2.6 copy.67
  268.7 30.9 %all_to_all.34 = bf16[2,6,640,80]{3,0,1,2:T(2,128)(2,1)S(1)} all-to-all(bf16[2,6,640,80]{3,0,1,2:T(2,128)(2,1)S(1)} %copy.67), channel_id=1, replica_groups=mesh['freq'=8,'panel'=16] {'panel'}, dimensions={2} | all-to-all | bytes 2457600 | tf_op jit(solution)/shard_map/all_to_all | solution.py:87
  299.5 0.4 copy.68
  299.9 0.3 copy.69
  300.3 0.9 slice-done.1
  301.4 4.0 %subtract_convert_fusion = bf16[40,80,1024]{2,1,0:T(8,128)(2,1)} fusion(bf16[40,80,1024]{2,1,0:T(8,128)(2,1)S(1)} %bitcast.142, bf16[192,40,80]{2,1,0:T(8,128)(2,1)S(1)} %bitcast.138, f32[96,1024]{1,0:T(8,128)S(1)} %copy-done.7, f32[96,1024]{1,0:T(8,128)S(1)} %copy-done.5), kind=kOutput, calls=%fused_computation | convolution fusion | flops 1272184832 | bytes 15122432 | tf_op jit(solution)/shard_map/csr,ct->srt/dot_general | solution.py:91
  (49 shorter events, 2.5 us)
Async XLA Ops:
  6.5 50.2 %copy-start = (f32[16,7,64]{2,0,1:T(8,128)S(1)}, f32[16,7,64]{2,0,1:T(8,128)}, u32[]{:S(2)}) copy-start(f32[16,7,64]{2,0,1:T(8,128)} %param.3) | copy-start | bytes 86020
  6.5 171.3 %all-gather.2.cloned.1.call-start = ((), (), s32[]{:S(2)}) async-start(), calls=%async_computation.2 | async-start | bytes 11059200 | tf_op jit(solution)/shard_map/all_gather | solution.py:74
  8.2 0.8 copy-start.4
  8.2 0.9 copy-start.6
  238.0 4.2 %copy-start.2 = (bf16[1,6,640,640]{3,2,1,0:T(8,128)(2,1)S(1)}, bf16[1,6,640,640]{3,2,1,0:T(8,128)(2,1)}, u32[]{:S(2)}) copy-start(bf16[1,6,640,640]{3,2,1,0:T(8,128)(2,1)} %copy.91) | copy-start | bytes 14745604
  242.2 2.4 copy-start.3
  268.6 31.6 %slice-start = ((s8[6553600]{0:T(1024)(128)(4,1)}), s8[4194304]{0:T(1024)(128)(4,1)S(1)}, s32[]{:S(2)}) async-start(s8[6553600]{0:T(1024)(128)(4,1)} %bitcast.141), calls=%async_computation.3 | async-start | bytes 8388608
  299.5 1.7 slice-start.1
  299.9 1.4 copy-start.5
  299.9 1.5 copy-start.7
  301.4 4.0 %copy-start.1 = (f32[16,7,64]{2,0,1:T(8,128)S(1)}, f32[16,7,64]{2,0,1:T(8,128)}, u32[]{:S(2)}) copy-start(f32[16,7,64]{2,0,1:T(8,128)} %param.3) | copy-start | bytes 86020
Sparse Core Ops, SparseCore 0:
  56.8 120.9 all-gather.1
where the time goes:
time: 314 us; the launch traced here: 312 us
  waiting for transfers between devices  119 us (38%)
  local copies, waits for them, and re-layouts  78.6 us (25%)
  blocking collectives  63.2 us (20%)
  matrix products  25 us (8%)
  between operations  13.7 us (4%)
  other arithmetic  13.1 us (4%)
    all_gather x1, waiting for transfers between devices, per_device(): complete = lax.all_gather(columns, 'freq', axis=3, tiled=True)  119 us
    unnamed x36, local copies, waits for them, and re-layouts  42.4 us
    all_to_all x1, blocking collectives, per_device(): lax.all_to_all(spectra, 'panel', split_axis=1, concat_axis=2, tiled=True)  32.3 us
    all_to_all x1, blocking collectives, per_device(): lax.all_to_all(matched.astype(jnp.bfloat16), 'panel', split_axis=2, conca...  30.9 us
    slice x1, local copies, waits for them, and re-layouts, complex_product(): left_side[0]  20.6 us
    dot_general x8, matrix products, factor_product(): jnp.einsum('gjo,god->gjd', leading_factor, trailing_factor, preferred_ele...  15.8 us
    another operation x2, other arithmetic  10.7 us
    all_to_all x3, local copies, waits for them, and re-layouts, per_device(): lax.all_to_all(spectra, 'panel', split_axis=1, concat_axis=2, tiled=True)  6.6 us
  transfers between devices with their start and end apart: 1, of which 1 were waited for; matrix products, arithmetic and copies ran while one was open for 1% of the time, Pallas kernels for 0%

commit v1 on v0

--- a/solution.py
+++ b/solution.py
@@ -71,7 +71,7 @@
     columns = lax.all_to_all(spectra, "panel", split_axis=1, concat_axis=2, tiled=True)
     slice_count = columns.shape[1]
     first_slice = lax.axis_index("panel") * slice_count
-    complete = lax.all_gather(columns, "freq", axis=3, tiled=True)
+    complete = jnp.concatenate(lax.all_gather(columns, "freq"), axis=3)
     order_one = (complex_product(complete, columns) / scale_sources).astype(jnp.bfloat16)
     order_two = complex_product(complete, order_one) / scale_sources
     prediction = (order_one.astype(jnp.float32) - order_two).astype(jnp.bfloat16)

time: 314 us -> 262 us (0.83)
  local copies, waits for them, and re-layouts: 78.6 us -> 32.8 us
  matrix products: 25 us -> 19.6 us
    unnamed x36 -> x32, local copies, waits for them, and re-layouts: 42.4 us -> 2.4 us
    slice x1, local copies, waits for them, and re-layouts: 20.6 us -> 6.98 us  [complex_product(): left_side[1]]
    all_gather x0 -> x2, local copies, waits for them, and re-layouts: none -> 12.4 us  [per_device(): complete = jnp.concatenate(lax.all_gather(columns, 'freq'), axis=3)]
    dot_general x8, matrix products: 15.8 us -> 10.4 us  [factor_product(): jnp.einsum('gjo,god->gjd', leading_factor, trailing_factor, preferred_ele...]
    all_to_all x3 -> x2, local copies, waits for them, and re-layouts: 6.6 us -> 2.07 us  [per_device(): lax.all_to_all(spectra, 'panel', split_axis=1, concat_axis=2, tiled=True)]
where the time goes in v1:
time: 262 us; the launch traced here: 261 us
  waiting for transfers between devices  119 us (45%)
  blocking collectives  63.2 us (24%)
  local copies, waits for them, and re-layouts  32.8 us (13%)
  matrix products  19.6 us (7%)
  between operations  13.8 us (5%)
  other arithmetic  13.3 us (5%)
    all_gather x1, waiting for transfers between devices, per_device(): complete = jnp.concatenate(lax.all_gather(columns, 'freq'), axis=3)  119 us
    all_to_all x1, blocking collectives, per_device(): lax.all_to_all(spectra, 'panel', split_axis=1, concat_axis=2, tiled=True)  32.3 us
    all_to_all x1, blocking collectives, per_device(): lax.all_to_all(matched.astype(jnp.bfloat16), 'panel', split_axis=2, conca...  30.9 us
    all_gather x2, local copies, waits for them, and re-layouts, per_device(): complete = jnp.concatenate(lax.all_gather(columns, 'freq'), axis=3)  12.4 us
    another operation x2, other arithmetic  10.9 us
    dot_general x8, matrix products, factor_product(): jnp.einsum('gjo,god->gjd', leading_factor, trailing_factor, preferred_ele...  10.4 us
    slice x1, local copies, waits for them, and re-layouts, complex_product(): left_side[1]  6.98 us
  transfers between devices with their start and end apart: 1, of which 1 were waited for; matrix products, arithmetic and copies ran while one was open for 1% of the time, Pallas kernels for 0%

profile of v1, /device:TPU:1, one launch (start us, length us, event | category | flops | bytes accessed | tf_op | source)
XLA Modules:
  0.0 261.3 jit_solution(4636179896849813843)
XLA Ops:
  6.5 1.6 fusion.24
  8.2 0.7 copy-done.3
  9.0 4.8 %convolution_convert_fusion = bf16[192,40,80]{0,2,1:T(8,128)(2,1)S(1)} fusion(bf16[40,80,1024]{2,1,0:T(8,128)(2,1)} %param.2, f32[96,1024]{1,0:T(8,128)S(1)} %get-tuple-element.24, f32[96,1024]{1,0:T(8,128)S(1)} %get-tuple-element.23), kind=kOutput, calls=%fused_computation.20 | convolution fusion | flops 1259495424 | bytes 8568832 | tf_op jit(solution)/shard_map/srt,ct->csr/dot_general | solution.py:69
  13.8 0.9 reshape.35
  14.7 3.3 %copy.55 = bf16[2,96,40,80]{3,2,0,1:T(8,128)(2,1)} copy(bf16[2,96,40,80]{1,0,3,2:T(2,128)(2,1)S(1)} %reshape.35) | data formatting | bytes 2457600 | tf_op jit(solution)/shard_map/reshape | solution.py:70
  18.0 32.3 %all_to_all.30 = bf16[2,96,40,80]{3,2,0,1:T(8,128)(2,1)S(1)} all-to-all(bf16[2,96,40,80]{3,2,0,1:T(8,128)(2,1)} %copy.55), channel_id=1, replica_groups=mesh['freq'=8,'panel'=16] {'panel'}, dimensions={1} | all-to-all | bytes 2457600 | tf_op jit(solution)/shard_map/all_to_all | solution.py:71
  50.4 1.7 copy.57
  52.1 3.7 %copy.58 = bf16[1,2,6,640,80]{3,4,2,1,0:T(8,128)(2,1)} copy(bf16[1,2,6,640,80]{4,3,2,1,0:T(8,128)(2,1)} %bitcast.128) | data formatting | bytes 2457600 | tf_op jit(solution)/shard_map/all_gather | solution.py:74
  56.5 0.2 fusion.9
  57.5 0.3 copy.56
  57.9 0.3 fusion.47
  58.4 118.6 %all-gather.2.cloned.1.call-done = bf16[8,2,6,640,80]{3,4,2,1,0:T(8,128)(2,1)} async-done(((bf16[1,2,6,640,80]{3,4,2,1,0:T(8,128)(2,1)}), bf16[8,2,6,640,80]{3,4,2,1,0:T(8,128)(2,1)}) %all-gather.2.cloned.1.call-update) | async-done | bytes 9830416 | tf_op jit(solution)/shard_map/all_gather | solution.py:74
  177.0 8.7 %copy.123 = bf16[8,2,6,640,80]{3,4,0,2,1:T(8,128)(2,1)} copy(bf16[8,2,6,640,80]{3,4,2,1,0:T(8,128)(2,1)} %all-gather.2.cloned.1.call-done) | data formatting | bytes 19660800 | tf_op jit(solution)/shard_map/all_gather | solution.py:74
  185.7 7.0 %fusion.46 = (bf16[1,6,640,8,80]{2,4,3,1,0:T(8,128)(2,1)S(1)}, bf16[1,6,640,8,80]{2,4,3,1,0:T(8,128)(2,1)}) fusion(bf16[2,6,640,8,80]{2,4,3,1,0:T(8,128)(2,1)} %bitcast.119), kind=kLoop, calls=%fused_computation.109 | loop fusion | bytes 19660800 | tf_op jit(solution)/shard_map/slice | solution.py:30
  192.7 3.5 %fusion.50 = f32[6,640,80]{1,2,0:T(8,128)S(1)} fusion(bf16[6,640,640]{1,2,0:T(8,128)(2,1)} %bitcast.115, bf16[6,640,80]{2,1,0:T(8,128)(2,1)S(1)} %bitcast.121), kind=kOutput, calls=%fused_computation.113 | convolution fusion | flops 393216000 | bytes 6758400 | tf_op jit(solution)/shard_map/gjo,god->gjd/dot_general | solution.py:25
  196.2 0.3 copy-done.2
  196.6 1.0 fusion.51
  197.5 1.0 fusion.4
  198.5 1.0 fusion.5
  199.8 1.0 fusion.11
  200.8 1.0 fusion.12
  201.8 1.0 fusion.6
  202.7 1.0 fusion.7
  203.7 0.4 fusion.8
  204.1 5.6 %subtract_convert_fusion.1 = bf16[1,6,640,80]{2,3,1,0:T(8,128)(2,1)S(1)} fusion(f32[2,6,640,80]{2,3,1,0:T(8,128)S(1)} %fusion.8, f32[6,80]{1,0:T(8,128)S(1)} %bitcast.153, f32[6,80]{1,0:T(8,128)S(1)} %bitcast.155, f32[6,80]{1,0:T(8,128)S(1)} %bitcast.157, f32[6,80]{1,0:T(8,128)S(1)} %bitcast.131, f32[6,80]{1,0:T(8,128)S(1)} %bitcast.133, ...), kind=kLoop, calls=%fused_computation.32 | loop fusion | flops 8601600 | bytes 5586944 | tf_op jit(solution)/shard_map/convert
  209.7 5.3 %add_convert_fusion = bf16[1,6,640,80]{2,3,1,0:T(8,128)(2,1)S(1)} fusion(f32[2,6,640,80]{2,3,1,0:T(8,128)S(1)} %fusion.8, f32[6,80]{1,0:T(8,128)S(1)} %bitcast.154, f32[6,80]{1,0:T(8,128)S(1)} %bitcast.156, f32[6,80]{1,0:T(8,128)S(1)} %bitcast.158, f32[6,80]{1,0:T(8,128)S(1)} %bitcast.132, f32[6,80]{1,0:T(8,128)S(1)} %bitcast.134, f32[6,80]{1,0:T(8,128)S(1)} %bitcast.136, ...), kind=kLoop, calls=%fused_computation.31 | loop fusion | flops 8601600 | bytes 5586944 | tf_op jit(solution)/shard_map/convert.1
  215.2 2.6 copy.75
  217.7 30.9 %all_to_all.31 = bf16[2,6,640,80]{3,0,1,2:T(2,128)(2,1)S(1)} all-to-all(bf16[2,6,640,80]{3,0,1,2:T(2,128)(2,1)S(1)} %copy.75), channel_id=1, replica_groups=mesh['freq'=8,'panel'=16] {'panel'}, dimensions={2} | all-to-all | bytes 2457600 | tf_op jit(solution)/shard_map/all_to_all | solution.py:87
  248.6 0.4 copy.76
  249.0 0.3 copy.77
  249.3 0.9 slice-done.1
  250.5 4.0 %subtract_convert_fusion = bf16[40,80,1024]{2,1,0:T(8,128)(2,1)} fusion(bf16[40,80,1024]{2,1,0:T(8,128)(2,1)S(1)} %bitcast.130, bf16[192,40,80]{2,1,0:T(8,128)(2,1)S(1)} %bitcast.126, f32[96,1024]{1,0:T(8,128)S(1)} %copy-done.6, f32[96,1024]{1,0:T(8,128)S(1)} %copy-done.4), kind=kOutput, calls=%fused_computation | convolution fusion | flops 1272184832 | bytes 15122432 | tf_op jit(solution)/shard_map/csr,ct->srt/dot_general | solution.py:91
  (46 shorter events, 2.2 us)
Async XLA Ops:
  6.5 49.3 %copy-start = (f32[16,7,64]{2,0,1:T(8,128)S(1)}, f32[16,7,64]{2,0,1:T(8,128)}, u32[]{:S(2)}) copy-start(f32[16,7,64]{2,0,1:T(8,128)} %param.3) | copy-start | bytes 86020
  6.5 170.5 %all-gather.2.cloned.1.call-start = ((), (), s32[]{:S(2)}) async-start(), calls=%async_computation.2 | async-start | bytes 11059200 | tf_op jit(solution)/shard_map/all_gather | solution.py:74
  8.2 0.7 copy-start.3
  8.2 0.9 copy-start.5
  192.7 3.9 %copy-start.2 = (bf16[1,6,640,8,80]{2,4,3,1,0:T(8,128)(2,1)S(1)}, bf16[1,6,640,8,80]{2,4,3,1,0:T(8,128)(2,1)}, u32[]{:S(2)}) copy-start(bf16[1,6,640,8,80]{2,4,3,1,0:T(8,128)(2,1)} %get-tuple-element.6) | copy-start | bytes 14745604
  217.7 31.6 %slice-start = ((s8[6553600]{0:T(1024)(128)(4,1)}), s8[4194304]{0:T(1024)(128)(4,1)S(1)}, s32[]{:S(2)}) async-start(s8[6553600]{0:T(1024)(128)(4,1)} %bitcast.129), calls=%async_computation.3 | async-start | bytes 8388608
  248.6 1.7 slice-start.1
  249.0 1.4 copy-start.4
  249.0 1.5 copy-start.6
  250.5 4.0 %copy-start.1 = (f32[16,7,64]{2,0,1:T(8,128)S(1)}, f32[16,7,64]{2,0,1:T(8,128)}, u32[]{:S(2)}) copy-start(f32[16,7,64]{2,0,1:T(8,128)} %param.3) | copy-start | bytes 86020
Sparse Core Ops, SparseCore 0:
  56.0 121.0 all-gather.1
